TPU v7x, 32 devices: a whole 2x2x4 slice. The times are simulated.
32 devices in a mesh: expert: 4 (over x, core), tensor: 8 (over z, y).
Axes of the slice: x: 2, y: 2, z: 4, core: 2. Of those that a mesh axis runs over, the one named last changes fastest.
Arguments:
- tokens: bfloat16 [128, 7168], P('expert', 'tensor'), may hold values from -6 to 6
- routes: int32 [128, 8], P('expert'), may hold values from 0 to 15, all different within a row; in each aligned block of 128 rows (0 to 127, 128 to 255, ...) at most 128 rows name the same one
- gates: bfloat16 [128, 8], P('expert'), may hold values from 0.099609375 to 0.59765625
- w_gate: bfloat16 [16, 2048, 7168], P('expert', 'tensor'), may hold values from -0.0625 to 0.0625
- w_up: bfloat16 [16, 2048, 7168], P('expert', 'tensor'), may hold values from -0.0625 to 0.0625
- w_down: bfloat16 [16, 2048, 7168], P('expert', None, 'tensor'), may hold values from -0.125 to 0.125
Outputs:
- moe_out: bfloat16 [128, 7168], P('expert', 'tensor')
Inputs may be any that keep to these rules, and one draw needn't show every extreme that they name: `routes`: each row names 8 different experts. No expert is named by more than 128 of the 128 rows, and one expert is named by exactly 128 rows.
All inputs are finite; a program needn't handle non-finite values.
Results may differ from a plain program's by a relative error of at most 0.0049.
Values may be sent and summed in bfloat16 or wider, within the bound.
A program may use at most 128 MiB of HBM per device.

v0:
```python
import jax
import jax.numpy as jnp
from jax import lax
from jax.sharding import PartitionSpec as P

CAP = 128


def entering(value, axis, combine, identity):
    length, index = (lax.axis_size(axis), lax.axis_index(axis))
    everything = lax.all_gather(value, axis)
    start = jnp.broadcast_to(jnp.asarray(identity, value.dtype), value.shape)

    def lap(k, before):
        reached = k < index
        new = combine(before, everything[k])
        return jnp.where(reached, new, before)

    return lax.fori_loop(0, length, lap, start)


def add_counts(earlier, later):
    return earlier + later


def on_device(tokens, routes, gates, w_gate, w_up, w_down):
    exp_dev = w_gate.shape[0]
    experts = exp_dev * lax.axis_size("expert")
    group_index = lax.axis_index("expert")
    expert_ids = jnp.arange(experts, dtype=jnp.int32)
    route_hits = routes[:, :, None] == expert_ids[None, None, :]
    member = jnp.sum(route_hits.astype(jnp.int32), axis=1)
    counts = jnp.sum(member, axis=0)
    offset = entering(counts, "expert", add_counts, jnp.zeros_like(counts))
    before = jnp.cumsum(member, axis=0) - member + offset[None, :]
    own_slot = jnp.sum(jnp.where(route_hits, before[:, None, :], 0), axis=2).astype(jnp.int32)
    all_routes, all_slots = (
        lax.all_gather(routes, "expert", axis=0, tiled=True),
        lax.all_gather(own_slot, "expert", axis=0, tiled=True),
    )
    row_block, all_gates = (
        lax.all_gather(tokens, "expert", axis=0, tiled=True),
        lax.all_gather(gates, "expert", axis=0, tiled=True),
    )
    gathered = lax.all_gather(row_block, "tensor", axis=1, tiled=True)
    local_ids = all_routes - group_index * exp_dev
    is_local = (local_ids >= 0) & (local_ids < exp_dev)
    slot_id = jnp.where(is_local, local_ids * CAP + all_slots, -1)
    slot_range = jnp.arange(exp_dev * CAP, dtype=jnp.int32)
    matches = slot_id[:, :, None] == slot_range[None, None, :]
    picked = jnp.any(matches, axis=1).astype(jnp.bfloat16)
    mixing = jnp.sum(jnp.where(matches, all_gates.astype(jnp.float32)[:, :, None], 0.0), axis=1)
    slot_rows = lax.dot_general(
        picked, gathered, (((0,), (0,)), ((), ())), preferred_element_type=jnp.float32
    ).astype(jnp.bfloat16)
    slot_rows = slot_rows.reshape(exp_dev, CAP, gathered.shape[1])
    gate_proj = jnp.einsum("ecd,efd->ecf", slot_rows, w_gate, preferred_element_type=jnp.float32)
    up_proj = jnp.einsum("ecd,efd->ecf", slot_rows, w_up, preferred_element_type=jnp.float32)
    hidden = (jax.nn.silu(gate_proj) * up_proj).astype(jnp.bfloat16)
    expert_out = jnp.einsum(
        "ecf,efd->ecd",
        lax.all_gather(hidden, "tensor", axis=2, tiled=True),
        w_down,
        preferred_element_type=jnp.float32,
    )
    expert_out = expert_out.reshape(exp_dev * CAP, w_down.shape[2])
    partial_value = jnp.dot(mixing, expert_out, precision=lax.Precision.HIGHEST)
    result = lax.psum_scatter(partial_value, "expert", scatter_dimension=0, tiled=True)
    return result.astype(jnp.bfloat16)


def solution(mesh):
    placed = (
        P("expert", "tensor"),
        P("expert", None),
        P("expert", None),
        P("expert", "tensor", None),
        P("expert", "tensor", None),
        P("expert", None, "tensor"),
    )
    return jax.shard_map(
        on_device, mesh=mesh, in_specs=placed, out_specs=P("expert", "tensor"), check_vma=False
    )
```

profile of v0, /device:TPU:0, one launch (start us, length us, event | category | flops | bytes accessed | tf_op | source)
XLA Modules:
  0.0 181.3 jit_solution(15544654380891682984)
XLA Ops:
  6.5 8.7 %all_gather.29 = bf16[128,896]{1,0:T(8,128)(2,1)} all-gather(bf16[32,896]{1,0:T(8,128)(2,1)} %param.8), channel_id=1, replica_groups=mesh['expert'=4,'tensor'=8] {'expert'}, dimensions={0}, use_global_device_ids=true | all-gather | bytes 286720 | tf_op jit(solution)/shard_map/all_gather | solution.py:42
  15.3 0.0 all-gather.7.cloned.1.call-update
  15.3 0.0 all-gather.9.cloned.1.call-start
  15.3 1.2 dynamic-slice
  17.2 0.8 convert_reduce_fusion
  18.0 0.2 dynamic-update-slice
  18.2 4.3 %all-reduce = s32[64]{0:T(128)S(1)} all-reduce(s32[64]{0:T(128)S(1)} %dynamic-update-slice), channel_id=2, replica_groups=mesh['expert'=4,'tensor'=8] {'expert'}, use_global_device_ids=true, to_apply=%add | all-reduce | flops 64 | bytes 512
  22.5 0.1 reshape.32
  22.6 0.1 copy.18
  22.6 0.1 reduce_window_sum.11
  22.7 0.1 while.14
  22.9 0.1 copy.20
  22.9 0.7 select_reduce_fusion.1
  23.7 5.2 %all-gather.2 = s32[4,32,8]{1,2,0:T(8,128)S(1)} all-gather(s32[1,32,8]{1,2,0:T(8,128)S(1)} %bitcast.29), channel_id=1, replica_groups=mesh['expert'=4,'tensor'=8] {'expert'}, dimensions={0}, use_global_device_ids=true | all-gather | bytes 5120 | tf_op jit(solution)/shard_map/all_gather | solution.py:39
  28.9 5.3 %all-gather.1 = s32[4,32,8]{1,2,0:T(8,128)S(1)} all-gather(s32[1,32,8]{1,2,0:T(8,128)} %bitcast.28), channel_id=1, replica_groups=mesh['expert'=4,'tensor'=8] {'expert'}, dimensions={0}, use_global_device_ids=true | all-gather | bytes 5120 | tf_op jit(solution)/shard_map/all_gather | solution.py:38
  34.2 0.1 copy.25
  34.3 0.7 fusion
  35.0 27.3 %all-gather.7.cloned.1.call-done = bf16[128,7168]{1,0:T(8,128)(2,1)} async-done(((bf16[128,896]{1,0:T(8,128)(2,1)}), bf16[128,7168]{1,0:T(8,128)(2,1)}) %all-gather.7.cloned.1.call-update) | async-done | bytes 1835024 | tf_op jit(solution)/shard_map/all_gather | solution.py:45
  62.3 6.6 %convolution_convert_fusion = bf16[512,7168]{1,0:T(8,128)(2,1)} fusion(pred[128,512]{1,0:T(8,128)(4,1)S(1)} %fusion, bf16[128,7168]{1,0:T(8,128)(2,1)} %all-gather.7.cloned.1.call-done), kind=kOutput, calls=%fused_computation.2 | convolution fusion | flops 943194112 | bytes 9240576 | tf_op jit(solution)/shard_map/dot_general | solution.py:53
  68.9 12.3 %fusion.2 = f32[4,128,256]{2,1,0:T(8,128)S(1)} fusion(bf16[4,128,7168]{2,1,0:T(8,128)(2,1)} %bitcast.22, bf16[4,256,7168]{2,1,0:T(8,128)(2,1)} %param.11), kind=kOutput, calls=%fused_computation.14 | convolution fusion | flops 1879048192 | bytes 22544384 | tf_op jit(solution)/shard_map/ecd,efd->ecf/dot_general | solution.py:57
  81.2 13.0 %fusion.1 = bf16[4,128,256]{2,1,0:T(8,128)(2,1)} fusion(bf16[4,128,7168]{2,1,0:T(8,128)(2,1)} %bitcast.23, bf16[4,256,7168]{2,1,0:T(8,128)(2,1)} %param.12, f32[4,128,256]{2,1,0:T(8,128)S(1)} %fusion.2), kind=kOutput, calls=%fused_computation.7 | convolution fusion | flops 1879834624 | bytes 22806528 | tf_op jit(solution)/shard_map/ecd,efd->ecf/dot_general | solution.py:58
  94.2 0.0 all-gather.9.cloned.1.call-update
  94.2 0.0 reduce-scatter.2.cloned.1.call-start
  94.3 5.4 %all-gather.3 = bf16[4,32,8]{1,2,0:T(8,128)(2,1)S(1)} all-gather(bf16[1,32,8]{1,2,0:T(8,128)(2,1)S(1)} %bitcast.30), channel_id=1, replica_groups=mesh['expert'=4,'tensor'=8] {'expert'}, dimensions={0}, use_global_device_ids=true | all-gather | bytes 2560 | tf_op jit(solution)/shard_map/all_gather | solution.py:43
  99.6 0.1 copy.26
  99.7 0.7 select_reduce_fusion
  100.4 43.1 %all-gather.9.cloned.1.call-done = bf16[4,128,2048]{2,1,0:T(8,128)(2,1)} async-done(((bf16[4,128,256]{2,1,0:T(8,128)(2,1)}), bf16[4,128,2048]{2,1,0:T(8,128)(2,1)}) %all-gather.9.cloned.1.call-update) | async-done | bytes 2097168 | tf_op jit(solution)/shard_map/all_gather | solution.py:62
  143.5 8.2 %fusion.3 = f32[4,128,896]{2,1,0:T(8,128)S(1)} fusion(bf16[4,128,2048]{2,1,0:T(8,128)(2,1)} %all-gather.9.cloned.1.call-done, bf16[4,2048,896]{2,1,0:T(8,128)(2,1)} %param.13), kind=kOutput, calls=%fused_computation.15 | convolution fusion | flops 1879048192 | bytes 18612224 | tf_op jit(solution)/shard_map/ecf,efd->ecd/dot_general | solution.py:60
  151.7 2.0 %fusion.4 = f32[128,896]{1,0:T(8,128)} fusion(f32[128,512]{1,0:T(8,128)S(1)} %select_reduce_fusion, f32[512,896]{1,0:T(8,128)S(1)} %bitcast.24), kind=kOutput, calls=%fused_computation.16 | convolution fusion | flops 704643072 | bytes 2555904 | tf_op jit(solution)/shard_map/dot_general | solution.py:67
  153.7 0.0 reduce-scatter.2.cloned.1.call-update
  153.7 19.5 %reduce-scatter.2.cloned.1.call-done = f32[32,896]{1,0:T(8,128)} async-done(((f32[128,896]{1,0:T(8,128)}), f32[32,896]{1,0:T(8,128)}) %reduce-scatter.2.cloned.1.call-update) | async-done | bytes 114704 | tf_op jit(solution)/shard_map/reduce_scatter | solution.py:68
  173.2 1.5 convert_element_type.20
  (11 shorter events, 0.1 us)
Async XLA Ops:
  6.5 55.8 %all-gather.7.cloned.1.call-start = ((), (), s32[]{:S(2)}) async-start(), calls=%async_computation.1 | async-start | bytes 2064384 | tf_op jit(solution)/shard_map/all_gather | solution.py:45
  15.3 128.3 %all-gather.9.cloned.1.call-start = ((), (), s32[]{:S(2)}) async-start(), calls=%async_computation.2 | async-start | bytes 2359296 | tf_op jit(solution)/shard_map/all_gather | solution.py:62
  81.2 13.1 %copy-start = (bf16[32,8]{0,1:T(8,128)(2,1)S(1)}, bf16[32,8]{0,1:T(8,128)(2,1)}, u32[]{:S(2)}) copy-start(bf16[32,8]{0,1:T(8,128)(2,1)} %param.10) | copy-start | bytes 1540
  94.2 79.0 %reduce-scatter.2.cloned.1.call-start = ((), (), s32[]{:S(2)}) async-start(), calls=%async_computation.3 | async-start | bytes 573440 | tf_op jit(solution)/shard_map/reduce_scatter | solution.py:68
Sparse Core Ops, SparseCore 0:
  15.4 46.8 all-gather.6
  94.3 49.1 all-gather.8
  153.8 19.3 reduce-scatter.1
where the time goes:
time: 182 us; the launch traced here: 181 us
  waiting for transfers between devices  90 us (49%)
  matrix products  42 us (23%)
  blocking collectives  28.9 us (16%)
  between operations  13.8 us (8%)
  other arithmetic  4.59 us (3%)
  local copies, waits for them, and re-layouts  1.88 us (1%)
    all_gather x1, waiting for transfers between devices, on_device(): lax.all_gather(hidden, 'tensor', axis=2, tiled=True)  43.1 us
    all_gather x1, waiting for transfers between devices, on_device(): gathered = lax.all_gather(row_block, 'tensor', axis=1, tiled=True)  27.3 us
    reduce_scatter x1, waiting for transfers between devices, on_device(): lax.psum_scatter(partial_value, 'expert', scatter_dimension=0, tiled=True)  19.5 us
    dot_general x1, matrix products, on_device(): jnp.einsum('ecd,efd->ecf', slot_rows, w_up, preferred_element_type=jnp.fl...  13 us
    dot_general x1, matrix products, on_device(): jnp.einsum('ecd,efd->ecf', slot_rows, w_gate, preferred_element_type=jnp....  12.3 us
    all_gather x1, blocking collectives, on_device(): lax.all_gather(tokens, 'expert', axis=0, tiled=True)  8.71 us
    dot_general x1, matrix products, on_device(): jnp.einsum('ecf,efd->ecd', lax.all_gather(hidden, 'tensor', axis=2, tiled...  8.16 us
    dot_general x1, matrix products, on_device(): lax.dot_general(picked, gathered, (((0,), (0,)), ((), ())), preferred_ele...  6.58 us
  transfers between devices with their start and end apart: 3, of which 3 were waited for; matrix products, arithmetic and copies ran while one was open for 3% of the time, Pallas kernels for 0%

commit v1 on v0

v1 whole, which is shorter than its diff:
```python
import functools

import jax
import jax.numpy as jnp
from jax import lax
from jax.experimental import pallas as pl
from jax.experimental.pallas import tpu as pltpu
from jax.sharding import PartitionSpec as P

MESH = pl.DeviceIdType.MESH
LANES = 128
TRANSPOSED = (((1,), (1,)), ((), ()))


def token_weights(routes, gates, width):
    ids = lax.broadcasted_iota(jnp.int32, (routes.shape[0], width), 1)
    total = jnp.zeros((routes.shape[0], width), jnp.float32)
    for k in range(routes.shape[1]):
        total += jnp.where(routes[:, k : k + 1] == ids, gates[:, k : k + 1].astype(jnp.float32), 0.0)
    return total


def kernel(
    groups, parts, tokens, routes, gates, w_gate, w_up, w_down, out,
    x_all, wts, wg, wu, wd, hid, g_acc, u_acc, acc, outgoing, incoming,
    own_sem, wg_sem, wu_sem, wd_sem,
    x_send, x_recv, w_send, w_recv, h_send, h_recv, r_send, r_recv,
):
    exp_dev, ff_blk, width = w_gate.shape
    rows, d_blk = tokens.shape
    n_x, n_z = groups // 2, parts // 2
    me_e, me_t = lax.axis_index("expert"), lax.axis_index("tensor")
    xi, ci, zi, yi = me_e // 2, me_e % 2, me_t // 2, me_t % 2

    def group_at(m, o):
        return lax.rem(xi + m, n_x) * 2 + (ci if o == 0 else 1 - ci)

    def part_at(k, o):
        return lax.rem(zi + k, n_z) * 2 + (yi if o == 0 else 1 - yi)

    def row_slice(g):
        return pl.ds(pl.multiple_of(g * rows, rows), rows)

    own = x_all.at[row_slice(me_e), pl.ds(pl.multiple_of(me_t * d_blk, LANES), d_blk)]
    own_copy = pltpu.make_async_copy(tokens, own, own_sem)
    own_copy.start()
    loads_g, loads_u, loads_d = [], [], []
    for e in range(exp_dev):
        loads_g.append(pltpu.make_async_copy(w_gate.at[e], wg.at[e], wg_sem.at[e]))
        loads_u.append(pltpu.make_async_copy(w_up.at[e], wu.at[e], wu_sem.at[e]))
        loads_d.append(pltpu.make_async_copy(w_down.at[e], wd.at[e], wd_sem.at[e]))
    for e in range(exp_dev):
        loads_g[e].start()
        loads_u[e].start()

    z_peers = [(me_e, part_at(k, 0)) for k in range(1, n_z)]
    y_peer = (me_e, part_at(0, 1))
    others = [(m, o) for m in range(n_x) for o in range(2) if (m, o) != (0, 0)]
    e_peers = [(group_at(m, o), me_t) for m, o in others]
    barrier = pltpu.get_barrier_semaphore()
    for peer in z_peers + [y_peer] + e_peers:
        pl.semaphore_signal(barrier, inc=1, device_id=peer, device_id_type=MESH)
    wts[row_slice(me_e), :] = token_weights(routes[...], gates[...], wts.shape[1])
    pl.semaphore_wait(barrier, len(z_peers) + 1 + len(e_peers))

    started = []

    def send(src, dst, send_sem, recv_sem, peer):
        copy = pltpu.make_async_remote_copy(
            src_ref=src, dst_ref=dst, send_sem=send_sem, recv_sem=recv_sem,
            device_id=peer, device_id_type=MESH,
        )
        copy.start()
        started.append(copy)

    def arrived(dst, recv_sem):
        pltpu.make_async_remote_copy(
            src_ref=dst, dst_ref=dst, send_sem=own_sem, recv_sem=recv_sem,
            device_id=y_peer, device_id_type=MESH,
        ).wait_recv()

    def block(m, o, k, yo):
        g, t = group_at(m, o), part_at(k, yo)
        return x_all.at[row_slice(g), pl.ds(pl.multiple_of(t * d_blk, LANES), d_blk)]

    def sem_z(k):
        return k - 1

    def sem_y(k):
        return n_z - 1 + k

    def sem_x(m, k, yo):
        return 2 * n_z - 1 + (m - 1) * parts + k * 2 + yo

    def sem_c(m, k, yo):
        return 2 * n_z - 1 + (n_x - 1) * parts + m * parts + k * 2 + yo

    def to_x(k, yo):
        b = block(0, 0, k, yo)
        for m in range(1, n_x):
            send(b, b, x_send.at[sem_x(m, k, yo)], x_recv.at[sem_x(n_x - m, k, yo)], (group_at(m, 0), me_t))

    def to_core(m, k, yo):
        b = block(m, 0, k, yo)
        s = sem_c(m, k, yo)
        send(b, b, x_send.at[s], x_recv.at[s], (group_at(0, 1), me_t))

    def to_y(k):
        b = block(0, 0, k, 0)
        send(b, b, x_send.at[sem_y(k)], x_recv.at[sem_y(k)], y_peer)

    own_copy.wait()
    first = block(0, 0, 0, 0)
    for k in range(1, n_z):
        send(first, first, x_send.at[sem_z(k)], x_recv.at[sem_z(n_z - k)], z_peers[k - 1])
    to_y(0)
    to_x(0, 0)
    to_core(0, 0, 0)
    mine = wts.at[row_slice(me_e), :]
    for (m, o), peer in zip(others, e_peers):
        back = ((n_x - m) % n_x) * 2 + o
        send(mine, mine, w_send.at[m * 2 + o], w_recv.at[back], peer)
    for e in range(exp_dev):
        loads_d[e].start()
    for k in range(1, n_z):
        arrived(block(0, 0, k, 0), x_recv.at[sem_z(k)])
        to_y(k)
        to_x(k, 0)
        to_core(0, k, 0)
    for k in range(n_z):
        arrived(block(0, 0, k, 1), x_recv.at[sem_y(k)])
        to_x(k, 1)
        to_core(0, k, 1)
    for yo in range(2):
        for k in range(n_z):
            for m in range(1, n_x):
                arrived(block(m, 0, k, yo), x_recv.at[sem_x(m, k, yo)])
                to_core(m, k, yo)
    for m, o in others:
        arrived(wts.at[row_slice(group_at(m, o)), :], w_recv.at[m * 2 + o])
    for m in range(n_x):
        for yo in range(2):
            for k in range(n_z):
                arrived(block(m, 1, k, yo), x_recv.at[sem_c(m, k, yo)])

    steps = 4 if width % (4 * 2 * LANES) == 0 else 1
    k_blk = width // steps

    def compute(e):
        loads_g[e].wait()
        loads_u[e].wait()
        g_acc[...] = jnp.zeros_like(g_acc)
        u_acc[...] = jnp.zeros_like(u_acc)

        def step(i, carry):
            cols = pl.ds(pl.multiple_of(i * k_blk, LANES), k_blk)
            x = x_all[:, cols]
            g_acc[...] += lax.dot_general(x, wg[e, :, cols], TRANSPOSED, preferred_element_type=jnp.float32)
            u_acc[...] += lax.dot_general(x, wu[e, :, cols], TRANSPOSED, preferred_element_type=jnp.float32)
            return carry

        lax.fori_loop(0, steps, step, 0)
        ids = lax.broadcasted_iota(jnp.int32, wts.shape, 1)
        weight = jnp.sum(jnp.where(ids == me_e * exp_dev + e, wts[...], 0.0), axis=1, keepdims=True)
        g = g_acc[...]
        hid[me_t, e] = (g / (1.0 + jnp.exp(-g)) * u_acc[...] * weight).astype(hid.dtype)

    def h_sem_z(k, e):
        return (k - 1) * exp_dev + e

    def h_sem_y(k, e):
        return (n_z - 1 + k) * exp_dev + e

    def h_to_y(k, e):
        b = hid.at[part_at(k, 0), e]
        send(b, b, h_send.at[h_sem_y(k, e)], h_recv.at[h_sem_y(k, e)], y_peer)

    def h_own(e):
        b = hid.at[me_t, e]
        h_to_y(0, e)
        for k in range(1, n_z):
            send(b, b, h_send.at[h_sem_z(k, e)], h_recv.at[h_sem_z(n_z - k, e)], z_peers[k - 1])

    def h_forward(e):
        for k in range(1, n_z):
            arrived(hid.at[part_at(k, 0), e], h_recv.at[h_sem_z(k, e)])
            h_to_y(k, e)

    def down(e, yo):
        def step(k, carry):
            t = lax.rem(zi + k, n_z) * 2 + (yi if yo == 0 else 1 - yi)
            w = wd[e, pl.ds(pl.multiple_of(t * ff_blk, ff_blk), ff_blk), :]
            acc[...] += jnp.dot(hid[t, e], w, preferred_element_type=jnp.float32)
            return carry

        lax.fori_loop(0, n_z, step, 0)

    def down_z(e):
        loads_d[e].wait()
        down(e, 0)

    def down_y(e):
        for k in range(n_z):
            arrived(hid.at[part_at(k, 1), e], h_recv.at[h_sem_y(k, e)])
        down(e, 1)

    acc[...] = jnp.zeros_like(acc)
    for e in range(exp_dev):
        compute(e)
        h_own(e)
        if e >= 2:
            h_forward(e - 2)
    late = range(max(exp_dev - 2, 0), exp_dev)
    for e in late:
        if e >= 2:
            down_z(e - 2)
        h_forward(e)
    for e in range(exp_dev):
        if e + 2 not in late:
            down_z(e)
    for e in range(exp_dev):
        down_y(e)

    for (m, o), peer in zip(others, e_peers):
        i = m * 2 + o
        outgoing[i] = acc[row_slice(group_at(m, o)), :].astype(outgoing.dtype)
        back = ((n_x - m) % n_x) * 2 + o
        send(outgoing.at[i], incoming.at[back], r_send.at[i], r_recv.at[back], peer)
    total = acc[row_slice(me_e), :]
    for m, o in others:
        arrived(incoming.at[m * 2 + o], r_recv.at[m * 2 + o])
    for m, o in others:
        total += incoming[m * 2 + o].astype(jnp.float32)
    out[...] = total.astype(out.dtype)
    for copy in started:
        copy.wait_send()


def fused(groups, parts, tokens, routes, gates, w_gate, w_up, w_down):
    exp_dev, ff_blk, width = w_gate.shape
    rows, d_blk = tokens.shape
    all_rows, experts = rows * groups, exp_dev * groups
    n_x, n_z = groups // 2, parts // 2
    x_copies = 2 * n_z - 1 + (n_x - 1) * parts + n_x * parts
    h_copies = (2 * n_z - 1) * exp_dev
    dma, kind = pltpu.SemaphoreType.DMA, tokens.dtype
    any_spec, vmem_spec = pl.BlockSpec(memory_space=pl.ANY), pl.BlockSpec(memory_space=pltpu.VMEM)
    return pl.pallas_call(
        functools.partial(kernel, groups, parts),
        out_shape=jax.ShapeDtypeStruct((rows, d_blk), kind),
        in_specs=[any_spec, vmem_spec, vmem_spec, any_spec, any_spec, any_spec],
        out_specs=vmem_spec,
        scratch_shapes=[
            pltpu.VMEM((all_rows, width), kind),
            pltpu.VMEM((all_rows, -(-experts // LANES) * LANES), jnp.float32),
            pltpu.VMEM(w_gate.shape, kind),
            pltpu.VMEM(w_up.shape, kind),
            pltpu.VMEM(w_down.shape, kind),
            pltpu.VMEM((parts, exp_dev, all_rows, ff_blk), kind),
            pltpu.VMEM((all_rows, ff_blk), jnp.float32),
            pltpu.VMEM((all_rows, ff_blk), jnp.float32),
            pltpu.VMEM((all_rows, d_blk), jnp.float32),
            pltpu.VMEM((groups, rows, d_blk), kind),
            pltpu.VMEM((groups, rows, d_blk), kind),
            dma, dma((exp_dev,)), dma((exp_dev,)), dma((exp_dev,)),
            dma((x_copies,)), dma((x_copies,)),
            dma((groups,)), dma((groups,)),
            dma((h_copies,)), dma((h_copies,)),
            dma((groups,)), dma((groups,)),
        ],
        compiler_params=pltpu.CompilerParams(
            collective_id=0, has_side_effects=True, vmem_limit_bytes=60 * 1024 * 1024
        ),
        name="moe_decode",
    )(tokens, routes, gates, w_gate, w_up, w_down)


def plain(groups, tokens, routes, gates, w_gate, w_up, w_down):
    exp_dev = w_gate.shape[0]
    weights = token_weights(routes, gates, exp_dev * groups)
    weights = lax.all_gather(weights, "expert", axis=0, tiled=True)
    own = lax.dynamic_slice_in_dim(weights, lax.axis_index("expert") * exp_dev, exp_dev, axis=1)
    row_block = lax.all_gather(tokens, "expert", axis=0, tiled=True)
    x = lax.all_gather(row_block, "tensor", axis=1, tiled=True)
    gate_proj = jnp.einsum("nd,efd->enf", x, w_gate, preferred_element_type=jnp.float32)
    up_proj = jnp.einsum("nd,efd->enf", x, w_up, preferred_element_type=jnp.float32)
    hidden = (jax.nn.silu(gate_proj) * up_proj * own.T[:, :, None]).astype(jnp.bfloat16)
    hidden = lax.all_gather(hidden, "tensor", axis=2, tiled=True)
    partial = jnp.einsum("enf,efd->nd", hidden, w_down, preferred_element_type=jnp.float32)
    return lax.psum_scatter(partial, "expert", scatter_dimension=0, tiled=True).astype(tokens.dtype)


def solution(mesh):
    groups, parts = mesh.shape["expert"], mesh.shape["tensor"]

    def on_device(tokens, routes, gates, w_gate, w_up, w_down):
        tiles = tokens.shape[1] % LANES == 0 and w_gate.shape[1] % LANES == 0 and tokens.shape[0] % 16 == 0
        if tiles and groups % 2 == 0 and parts % 2 == 0:
            return fused(groups, parts, tokens, routes, gates, w_gate, w_up, w_down)
        return plain(groups, tokens, routes, gates, w_gate, w_up, w_down)

    placed = (
        P("expert", "tensor"),
        P("expert", None),
        P("expert", None),
        P("expert", "tensor", None),
        P("expert", "tensor", None),
        P("expert", None, "tensor"),
    )
    return jax.shard_map(
        on_device, mesh=mesh, in_specs=placed, out_specs=P("expert", "tensor"), check_vma=False
    )
```

time: 182 us -> 72.3 us (0.40)
  the two profiles are of different devices: /device:TPU:0 before, /device:TPU:11 now
where the time goes in v1:
time: 72.3 us; the launch traced here: 71.9 us
  Pallas kernels  67.7 us (94%)
  local copies, waits for them, and re-layouts  4.16 us (6%)
    pallas_call x1, Pallas kernels, fused(): pl.pallas_call(functools.partial(kernel, groups, parts), out_shape=jax.Sh...  67.7 us
    unnamed x3, local copies, waits for them, and re-layouts  4.16 us

profile of v1, /device:TPU:11, one launch (start us, length us, event | category | flops | bytes accessed | tf_op | source)
XLA Modules:
  0.0 71.9 jit_solution(9110258023643607780)
XLA Ops:
  0.0 1.3 %copy.8.gates = bf16[32,8]{1,0:T(8,128)(2,1)} copy(bf16[32,8]{0,1:T(8,128)(2,1)} %param.8) | data formatting | bytes 1024 | tf_op args[2]
  1.4 1.4 %copy.7.routes = s32[32,8]{1,0:T(8,128)} copy(s32[32,8]{0,1:T(8,128)} %param.7) | data formatting | bytes 2048 | tf_op args[1]
  2.7 67.7 %moe_decode.1 = bf16[32,896]{1,0:T(8,128)(2,1)} custom-call(bf16[32,896]{1,0:T(8,128)(2,1)} %tokens.1, s32[32,8]{1,0:T(8,128)} %copy.7.routes, bf16[32,8]{1,0:T(8,128)(2,1)} %copy.8.gates, bf16[4,256,7168]{2,1,0:T(8,128)(2,1)} %w_gate.1, bf16[4,256,7168]{2,1,0:T(8,128)(2,1)} %w_up.1, bf16[4,2048,896]{2,1,0:T(8,128)(2,1)} %w_down.1), custom_call_target="tpu_custom_call" | custom-call | tf_op jit(solution)/shard_map/moe_decode/pallas_call | solution.py:248
  70.5 1.4 %copy.10 = bf16[32,896]{1,0:T(8,128)(2,1)} copy(bf16[32,896]{1,0:T(8,128)(2,1)} %moe_decode.1) | data formatting | bytes 114688

commit v2 on v1

--- a/solution.py
+++ b/solution.py
@@ -29,6 +29,7 @@
     exp_dev, ff_blk, width = w_gate.shape
     rows, d_blk = tokens.shape
     n_x, n_z = groups // 2, parts // 2
+    bits = [1 << i for i in range((n_z - 1).bit_length())]
     me_e, me_t = lax.axis_index("expert"), lax.axis_index("tensor")
     xi, ci, zi, yi = me_e // 2, me_e % 2, me_t // 2, me_t % 2
 
@@ -36,7 +37,11 @@
         return lax.rem(xi + m, n_x) * 2 + (ci if o == 0 else 1 - ci)
 
     def part_at(k, o):
-        return lax.rem(zi + k, n_z) * 2 + (yi if o == 0 else 1 - yi)
+        z = zi
+        for bit in bits:
+            if k & bit:
+                z = z + bit - 2 * bit * ((zi // bit) % 2)
+        return z * 2 + (yi if o == 0 else 1 - yi)
 
     def row_slice(g):
         return pl.ds(pl.multiple_of(g * rows, rows), rows)
@@ -112,7 +117,7 @@
     own_copy.wait()
     first = block(0, 0, 0, 0)
     for k in range(1, n_z):
-        send(first, first, x_send.at[sem_z(k)], x_recv.at[sem_z(n_z - k)], z_peers[k - 1])
+        send(first, first, x_send.at[sem_z(k)], x_recv.at[sem_z(k)], z_peers[k - 1])
     to_y(0)
     to_x(0, 0)
     to_core(0, 0, 0)
@@ -178,17 +183,33 @@
     def h_own(e):
         b = hid.at[me_t, e]
         h_to_y(0, e)
-        for k in range(1, n_z):
-            send(b, b, h_send.at[h_sem_z(k, e)], h_recv.at[h_sem_z(n_z - k, e)], z_peers[k - 1])
+        for k in reversed(bits):
+            h_to_z(b, k, k, e)
+
+    def h_to_z(b, step, role, e):
+        s = h_sem_z(role, e)
+        send(b, b, h_send.at[s], h_recv.at[s], z_peers[step - 1])
+
+    def h_take(k, e):
+        b = hid.at[part_at(k, 0), e]
+        arrived(b, h_recv.at[h_sem_z(k, e)])
+        for bit in reversed(bits):
+            if bit < (k & -k):
+                h_to_z(b, bit, k | bit, e)
+        h_to_y(k, e)
+
+    def h_relay(e):
+        for k in reversed(bits):
+            h_take(k, e)
 
     def h_forward(e):
-        for k in range(1, n_z):
-            arrived(hid.at[part_at(k, 0), e], h_recv.at[h_sem_z(k, e)])
-            h_to_y(k, e)
+        for k in sorted(range(1, n_z), key=lambda k: -(k & -k)):
+            if k not in bits:
+                h_take(k, e)
 
     def down(e, yo):
         def step(k, carry):
-            t = lax.rem(zi + k, n_z) * 2 + (yi if yo == 0 else 1 - yi)
+            t = k * 2 + (yi if yo == 0 else 1 - yi)
             w = wd[e, pl.ds(pl.multiple_of(t * ff_blk, ff_blk), ff_blk), :]
             acc[...] += jnp.dot(hid[t, e], w, preferred_element_type=jnp.float32)
             return carry
@@ -208,16 +229,17 @@
     for e in range(exp_dev):
         compute(e)
         h_own(e)
+        if e >= 1:
+            h_relay(e - 1)
         if e >= 2:
             h_forward(e - 2)
-    late = range(max(exp_dev - 2, 0), exp_dev)
-    for e in late:
-        if e >= 2:
-            down_z(e - 2)
-        h_forward(e)
-    for e in range(exp_dev):
-        if e + 2 not in late:
-            down_z(e)
+    h_relay(exp_dev - 1)
+    if exp_dev >= 2:
+        h_forward(exp_dev - 2)
+    for e in range(exp_dev - 1):
+        down_z(e)
+    h_forward(exp_dev - 1)
+    down_z(exp_dev - 1)
     for e in range(exp_dev):
         down_y(e)
 
@@ -295,7 +317,7 @@
 
     def on_device(tokens, routes, gates, w_gate, w_up, w_down):
         tiles = tokens.shape[1] % LANES == 0 and w_gate.shape[1] % LANES == 0 and tokens.shape[0] % 16 == 0
-        if tiles and groups % 2 == 0 and parts % 2 == 0:
+        if tiles and groups % 2 == 0 and parts > 1 and parts & (parts - 1) == 0:
             return fused(groups, parts, tokens, routes, gates, w_gate, w_up, w_down)
         return plain(groups, tokens, routes, gates, w_gate, w_up, w_down)
 

time: 72.3 us -> 66.8 us (0.924)
  the two profiles are of different devices: /device:TPU:11 before, /device:TPU:0 now
where the time goes in v2:
time: 66.8 us; the launch traced here: 66.4 us
  Pallas kernels  62.2 us (93%)
  local copies, waits for them, and re-layouts  4.16 us (6%)
    pallas_call x1, Pallas kernels, fused(): pl.pallas_call(functools.partial(kernel, groups, parts), out_shape=jax.Sh...  62.2 us
    unnamed x3, local copies, waits for them, and re-layouts  4.16 us

profile of v2, /device:TPU:0, one launch (start us, length us, event | category | flops | bytes accessed | tf_op | source)
XLA Modules:
  0.0 66.4 jit_solution(5699140041691641783)
XLA Ops:
  0.0 1.3 %copy.8.gates = bf16[32,8]{1,0:T(8,128)(2,1)} copy(bf16[32,8]{0,1:T(8,128)(2,1)} %param.8) | data formatting | bytes 1024 | tf_op args[2]
  1.4 1.4 %copy.7.routes = s32[32,8]{1,0:T(8,128)} copy(s32[32,8]{0,1:T(8,128)} %param.7) | data formatting | bytes 2048 | tf_op args[1]
  2.7 62.2 %moe_decode.1 = bf16[32,896]{1,0:T(8,128)(2,1)} custom-call(bf16[32,896]{1,0:T(8,128)(2,1)} %tokens.1, s32[32,8]{1,0:T(8,128)} %copy.7.routes, bf16[32,8]{1,0:T(8,128)(2,1)} %copy.8.gates, bf16[4,256,7168]{2,1,0:T(8,128)(2,1)} %w_gate.1, bf16[4,256,7168]{2,1,0:T(8,128)(2,1)} %w_up.1, bf16[4,2048,896]{2,1,0:T(8,128)(2,1)} %w_down.1), custom_call_target="tpu_custom_call" | custom-call | tf_op jit(solution)/shard_map/moe_decode/pallas_call | solution.py:270
  65.0 1.4 %copy.10 = bf16[32,896]{1,0:T(8,128)(2,1)} copy(bf16[32,896]{1,0:T(8,128)(2,1)} %moe_decode.1) | data formatting | bytes 114688
